TPU v7x, 32 devices: a whole 2x2x4 slice. The times are simulated.
32 devices in a mesh: seq: 4 (over z), chan: 8 (over y, x, core).
Axes of the slice: x: 2, y: 2, z: 4, core: 2. Of those that a mesh axis runs over, the one named last changes fastest.
Arguments:
- tokens: bfloat16 [4096, 4096], P('seq', 'chan'), may hold values from -8 to 8
- norm_gain: float32 [4096], replicated, may hold values from 0.5 to 1.5
- gate_proj: bfloat16 [4096, 8192], P(None, 'chan'), may hold values from -0.09375 to 0.09375
- inner_proj: bfloat16 [4096, 8192], P(None, 'chan'), may hold values from -0.09375 to 0.09375
- state_proj: bfloat16 [4096, 384], P('chan'), may hold values from -0.11816406 to 0.11816406
- conv_inner: float32 [4, 8192], P(None, 'chan'), may hold values from -3 to 3
- conv_state: float32 [4, 256], replicated, may hold values from -3 to 3
- log_rate: float32 [128], P('chan'), may hold values from -1 to 0
- rate_bias: float32 [128], P('chan'), may hold values from -16 to -2
- skip_gain: float32 [128], P('chan'), may hold values from 0.2 to 4
- gate_gain: float32 [8192], P('chan'), may hold values from 0.5 to 1.5
- out_proj: bfloat16 [8192, 4096], P('chan'), may hold values from -0.09375 to 0.09375
Outputs:
- layer_out: bfloat16 [4096, 4096], P('seq', 'chan')
All inputs are finite; a program needn't handle non-finite values.
Results may differ from a plain program's by a relative error of at most 0.012.
Values may be sent and summed in bfloat16 or wider, within the bound.
A program may use at most 128 MiB of HBM per device.

v0:
```python
import jax
import jax.numpy as jnp
from jax import lax
from jax.sharding import PartitionSpec as P

P_SIZE = 64
N = 128
K = 4
Q = 256
DI = 8192
precise = lax.Precision.HIGHEST


def from_behind(value, axis, steps):
    count = lax.axis_size(axis)
    leading, last = (max(0, -steps), min(count, count - steps))
    return lax.ppermute(value, axis, [(source, source + steps) for source in range(leading, last)])


def causal_mix(rim_part, fresh_rows, weights):
    length = fresh_rows.shape[0]
    padded = jnp.concatenate([rim_part.astype(jnp.float32), fresh_rows.astype(jnp.float32)], axis=0)
    summed = jnp.zeros(fresh_rows.shape, jnp.float32)
    for offset in range(weights.shape[0]):
        summed = summed + weights[offset] * padded[offset : offset + length]
    return jax.nn.silu(summed)


def local(
    tokens,
    norm_gain,
    gate_proj,
    inner_proj,
    state_proj,
    conv_inner,
    conv_state,
    log_rate,
    rate_bias,
    skip_gain,
    gate_gain,
    out_proj,
):
    gathered = lax.all_gather(tokens, "chan", axis=1, tiled=True)
    widened = gathered.astype(jnp.float32)
    inverse = lax.rsqrt(jnp.mean(widened * widened, axis=1, keepdims=True) + 1e-05)
    normed = (widened * inverse * norm_gain).astype(jnp.bfloat16)
    gate_raw = jnp.dot(normed, gate_proj, preferred_element_type=jnp.float32).astype(jnp.bfloat16)
    inner_raw = jnp.dot(normed, inner_proj, preferred_element_type=jnp.float32).astype(jnp.bfloat16)
    heads = log_rate.shape[0]
    start_head = lax.axis_index("chan") * heads
    projected = jnp.dot(
        normed,
        lax.all_gather(state_proj, "chan", axis=0, tiled=True),
        preferred_element_type=jnp.float32,
    )
    state_raw = projected[:, : 2 * N]
    raw_rate = lax.dynamic_slice_in_dim(projected, 2 * N + start_head, heads, 1)
    rim_rows = from_behind(
        (inner_raw[-(K - 1) :].astype(jnp.float32), state_raw[-(K - 1) :]), "seq", 1
    )
    inner_conv = causal_mix(rim_rows[0].astype(jnp.bfloat16), inner_raw, conv_inner)
    state_conv = causal_mix(rim_rows[1], state_raw, conv_state)
    token_rows = tokens.shape[0]
    blocks = token_rows // Q
    step_size = jax.nn.softplus(raw_rate + rate_bias)
    decay_log = -jnp.exp(log_rate) * step_size
    values = inner_conv.reshape(blocks, Q, heads, P_SIZE)
    in_map = state_conv[:, :N].reshape(blocks, Q, N)
    out_map = state_conv[:, N:].reshape(blocks, Q, N)
    step_rows = step_size.reshape(blocks, Q, heads).transpose(0, 2, 1)
    log_rows = decay_log.reshape(blocks, Q, heads).transpose(0, 2, 1)
    lower_mask = (jnp.arange(Q)[:, None] >= jnp.arange(Q)[None, :]).astype(jnp.float32)
    within = jnp.einsum("chs,ts->cht", log_rows, lower_mask, precision=precise)
    log_gaps = within[..., :, None] - within[..., None, :]
    fading = jnp.exp(jnp.where(lower_mask > 0, log_gaps, -jnp.inf))
    scores = jnp.einsum("ctn,csn->cts", out_map, in_map, precision=precise)
    mixing = scores[:, None] * fading * step_rows[:, :, None, :]
    local_out = jnp.einsum("chts,cshp->cthp", mixing, values, precision=precise)
    tail_weight = jnp.exp(within[..., -1:] - within) * step_rows
    scaled = values * tail_weight.transpose(0, 2, 1)[..., None]
    block_end = jnp.einsum("csn,cshp->chnp", in_map, scaled, precision=precise)
    block_log = within[..., -1]
    through = jnp.cumsum(block_log, axis=0)
    before = through - block_log
    earlier = jnp.arange(blocks)[:, None] > jnp.arange(blocks)[None, :]
    passage = jnp.exp(
        jnp.where(earlier[:, :, None], before[:, None, :] - through[None, :, :], -jnp.inf)
    )
    entering = jnp.einsum("cdh,dhnp->chnp", passage, block_end, precision=precise)
    device_end = jnp.einsum(
        "ch,chnp->hnp", jnp.exp(through[-1:] - through), block_end, precision=precise
    )
    device_fade = jnp.exp(through[-1])

    def hand_on(turn_index, incoming):
        return from_behind(device_fade[:, None, None] * incoming + device_end, "seq", 1)

    carried = lax.fori_loop(0, lax.axis_size("seq") - 1, hand_on, jnp.zeros_like(device_end))
    entering = entering + jnp.exp(before)[:, :, None, None] * carried[None]
    carried_out = jnp.einsum("ctn,chnp->cthp", out_map, entering, precision=precise)
    carried_out = carried_out * jnp.exp(within).transpose(0, 2, 1)[..., None]
    skip_wide = jnp.repeat(skip_gain, P_SIZE)
    ssd_out = (local_out + carried_out).reshape(token_rows, heads * P_SIZE) + skip_wide * inner_conv
    gated_out = ssd_out * jax.nn.silu(gate_raw.astype(jnp.float32))
    energy = lax.psum(jnp.sum(gated_out * gated_out, axis=1), "chan")
    norm_scale = lax.rsqrt(energy / DI + 1e-05)
    shaped = (gated_out * norm_scale[:, None] * gate_gain).astype(jnp.bfloat16)
    partial_out = jnp.dot(shaped, out_proj, preferred_element_type=jnp.float32)
    summed = lax.psum_scatter(partial_out, "chan", scatter_dimension=1, tiled=True)
    return (tokens.astype(jnp.float32) + summed).astype(jnp.bfloat16)


def solution(mesh):
    return jax.shard_map(
        local,
        mesh=mesh,
        in_specs=(
            P("seq", "chan"),
            P(),
            P(None, "chan"),
            P(None, "chan"),
            P("chan", None),
            P(None, "chan"),
            P(),
            P("chan"),
            P("chan"),
            P("chan"),
            P("chan"),
            P("chan", None),
        ),
        out_specs=P("seq", "chan"),
        check_vma=False,
    )
```

profile of v0, /device:TPU:0, one launch (start us, length us, event | category | flops | bytes accessed | tf_op | source)
XLA Modules:
  0.0 420.9 jit_solution(6865665323999386071)
XLA Ops:
  9.6 0.8 fusion.72
  10.4 0.9 fusion.71
  11.3 56.5 %all-gather.3.cloned.1.call-done = bf16[1024,4096]{1,0:T(8,128)(2,1)} async-done(((bf16[1024,512]{1,0:T(8,128)(2,1)}), bf16[1024,4096]{1,0:T(8,128)(2,1)}) %all-gather.3.cloned.1.call-update) | async-done | bytes 8388624 | tf_op jit(solution)/shard_map/all_gather | solution.py:43
  67.8 5.1 %fusion = f32[1024]{0:T(1024)S(1)} fusion(bf16[1024,4096]{1,0:T(8,128)(2,1)} %all-gather.3.cloned.1.call-done), kind=kLoop, calls=%fused_computation.3 | loop fusion | flops 12581888 | bytes 8392704 | tf_op jit(solution)/shard_map/reduce_sum | solution.py:45
  72.9 29.0 %all-gather.5.cloned.1.call-done = bf16[4096,384]{1,0:T(8,128)(2,1)} async-done(((bf16[512,384]{1,0:T(8,128)(2,1)}), bf16[4096,384]{1,0:T(8,128)(2,1)}) %all-gather.5.cloned.1.call-update) | async-done | bytes 3145744 | tf_op jit(solution)/shard_map/all_gather | solution.py:53
  101.9 8.1 %fusion.66 = f32[1024,384]{1,0:T(8,128)S(1)} fusion(bf16[4096,384]{1,0:T(8,128)(2,1)} %all-gather.5.cloned.1.call-done, bf16[1024,4096]{1,0:T(8,128)(2,1)} %all-gather.3.cloned.1.call-done, f32[4096]{0:T(1024)S(1)} %copy-done.4, f32[1024]{0:T(1024)S(1)} %add_rsqrt_fusion.1), kind=kOutput, calls=%fused_computation.96 | convolution fusion | flops 3238002688 | bytes 13127680 | tf_op jit(solution)/shard_map/dot_general | solution.py:51
  111.4 15.2 %fusion.73 = (f32[1024,1024]{1,0:T(8,128)}, bf16[1024,1024]{1,0:T(8,128)(2,1)S(1)}) fusion(bf16[4096,1024]{1,0:T(8,128)(2,1)} %param.17, bf16[1024,4096]{1,0:T(8,128)(2,1)} %all-gather.3.cloned.1.call-done, f32[4096]{0:T(1024)S(1)} %copy-done.4, f32[1024]{0:T(1024)S(1)} %add_rsqrt_fusion.1), kind=kOutput, calls=%fused_computation.101 | convolution fusion | flops 8608808960 | bytes 23089152 | tf_op jit(solution)/shard_map/dot_general | solution.py:48
  126.6 3.4 collective-permute-start.1
  130.0 3.9 collective-permute-start.2
  135.4 1.0 fusion.74
  136.5 3.9 divide_multiply_fusion
  140.3 5.3 %copy.47 = f32[1024,1024]{0,1:T(8,128)} copy(f32[1024,1024]{1,0:T(8,128)} %divide_multiply_fusion) | data formatting | bytes 8388608 | tf_op jit(solution)/shard_map/jit(silu)/mul | solution.py:26
  145.7 5.6 %reshape.68 = f32[4,256,16,64]{1,0,3,2:T(4,128)} reshape(f32[1024,1024]{0,1:T(8,128)} %copy.47) | data formatting | bytes 8388608 | tf_op jit(solution)/shard_map/reshape | solution.py:67
  151.3 3.3 broadcast_multiply_fusion
  154.7 5.4 %fusion.31 = (f32[16,128,64]{1,2,0:T(8,128)S(1)}, f32[4,16,64,128]{3,2,1,0:T(8,128)}) fusion(f32[16,4]{0,1:T(4,128)S(1)} %get-tuple-element.50, f32[4,256,128,1]{2,1,3,0:T(8,128)S(1)} %bitcast.77, f32[4,256,16,64]{1,0,3,2:T(4,128)S(1)} %broadcast_multiply_fusion), kind=kOutput, calls=%fused_computation.44 | convolution fusion | flops 1611530240 | bytes 7340288 | tf_op jit(solution)/shard_map/csn,cshp->chnp/dot_general | solution.py:81
  160.1 41.4 %while.10 = (s32[]{:T(128)}, f32[16,128,64]{1,2,0:T(8,128)S(1)}, f32[16]{0:T(128)S(1)}, f32[16,128,64]{1,2,0:T(8,128)S(1)}, s32[]{:T(128)}) while((s32[]{:T(128)}, f32[16,128,64]{1,2,0:T(8,128)S(1)}, f32[16]{0:T(128)S(1)}, f32[16,128,64]{1,2,0:T(8,128)S(1)}, s32[]{:T(128)}) %tuple.31), condition=%wide.region_3.4_spmd, body=%wide.region_2.3_spmd.sunk | while | flops 262146 | bytes 3670181 | solution.py:98
  160.3 4.2 %collective-permute-start = (f32[16,128,64]{1,2,0:T(8,128)S(1)}, f32[16,128,64]{1,2,0:T(8,128)S(1)}, u32[]{:S(2)}, u32[]{:S(2)}) collective-permute-start(f32[16,128,64]{1,2,0:T(8,128)S(1)} %multiply_add_fusion.2), channel_id=1, source_target_pairs={{0,8},{8,16},{16,24},{1,9},{9,17},{17,25},{2,10},{10,18},{18,26},{... | collective-permute-start | bytes 1572872 | tf_op jit(solution)/shard_map/while/body/eval_jaxpr/ppermute | solution.py:17
  164.5 10.1 %collective-permute-done = f32[16,128,64]{1,2,0:T(8,128)S(1)} collective-permute-done((f32[16,128,64]{1,2,0:T(8,128)S(1)}, f32[16,128,64]{1,2,0:T(8,128)S(1)}, u32[]{:S(2)}, u32[]{:S(2)}) %collective-permute-start) | collective-permute-done | bytes 524320 | tf_op jit(solution)/shard_map/while/body/eval_jaxpr/ppermute | solution.py:17
  174.7 4.4 %collective-permute-start = (f32[16,128,64]{1,2,0:T(8,128)S(1)}, f32[16,128,64]{1,2,0:T(8,128)S(1)}, u32[]{:S(2)}, u32[]{:S(2)}) collective-permute-start(f32[16,128,64]{1,2,0:T(8,128)S(1)} %multiply_add_fusion.2), channel_id=1, source_target_pairs={{0,8},{8,16},{16,24},{1,9},{9,17},{17,25},{2,10},{10,18},{18,26},{... | collective-permute-start | bytes 1572872 | tf_op jit(solution)/shard_map/while/body/eval_jaxpr/ppermute | solution.py:17
  179.2 9.2 %collective-permute-done = f32[16,128,64]{1,2,0:T(8,128)S(1)} collective-permute-done((f32[16,128,64]{1,2,0:T(8,128)S(1)}, f32[16,128,64]{1,2,0:T(8,128)S(1)}, u32[]{:S(2)}, u32[]{:S(2)}) %collective-permute-start) | collective-permute-done | bytes 524320 | tf_op jit(solution)/shard_map/while/body/eval_jaxpr/ppermute | solution.py:17
  188.5 4.4 %collective-permute-start = (f32[16,128,64]{1,2,0:T(8,128)S(1)}, f32[16,128,64]{1,2,0:T(8,128)S(1)}, u32[]{:S(2)}, u32[]{:S(2)}) collective-permute-start(f32[16,128,64]{1,2,0:T(8,128)S(1)} %multiply_add_fusion.2), channel_id=1, source_target_pairs={{0,8},{8,16},{16,24},{1,9},{9,17},{17,25},{2,10},{10,18},{18,26},{... | collective-permute-start | bytes 1572872 | tf_op jit(solution)/shard_map/while/body/eval_jaxpr/ppermute | solution.py:17
  192.9 8.4 %collective-permute-done = f32[16,128,64]{1,2,0:T(8,128)S(1)} collective-permute-done((f32[16,128,64]{1,2,0:T(8,128)S(1)}, f32[16,128,64]{1,2,0:T(8,128)S(1)}, u32[]{:S(2)}, u32[]{:S(2)}) %collective-permute-start) | collective-permute-done | bytes 524320 | tf_op jit(solution)/shard_map/while/body/eval_jaxpr/ppermute | solution.py:17
  201.5 6.7 %bitcast_add_fusion.1 = f32[4,16,128,64]{2,0,3,1:T(4,128)S(1)} fusion(f32[4,16,128,64]{2,3,1,0:T(8,128)} %bitcast.72, f32[16,128,64]{1,2,0:T(8,128)S(1)} %get-tuple-element.27, f32[4,16]{0,1:T(8,128)S(1)} %copy.58, f32[4,16]{0,1:T(8,128)S(1)} %copy.56, f32[4,16]{0,1:T(8,128)S(1)} %copy.55, pred[4,4]{1,0:T(4,128)(4,1)S(1)} %iota_compare_fusion.1), kind=kOutput, calls=%fused_computation.45 | convolution fusion | flops 26214912 | bytes 4719376 | tf_op jit(solution)/shard_map/cdh,dhnp->chnp/dot_general | solution.py:89
  208.5 3.5 fusion.75
  212.0 20.5 %bitcast_add_fusion = f32[4,256,16,64]{1,3,2,0:T(8,128)} fusion(f32[4,256,16,64]{1,3,2,0:T(8,128)S(1)} %bitcast.78, f32[4,256,16]{1,2,0:T(8,128)S(1)} %exponential_bitcast_fusion, f32[4,16,256]{2,1,0:T(8,128)S(1)} %copy.50, f32[4,16,256]{2,1,0:T(8,128)S(1)} %fusion.51, f32[4,256,256]{2,1,0:T(8,128)S(1)} %fusion.74, ...), kind=kOutput, calls=%fused_computation.35 | convolution fusion | flops 3240099840 | bytes 13893632 | tf_op jit(solution)/shard_map/chts,cshp->cthp/dot_general | solution.py:78
  232.6 8.1 %copy.71 = f32[4,256,16,64]{3,2,1,0:T(8,128)} copy(f32[4,256,16,64]{1,3,2,0:T(8,128)} %bitcast_add_fusion) | data formatting | bytes 8388608 | tf_op jit(solution)/shard_map/reshape | solution.py:103
  240.6 7.7 %reshape.81 = f32[1024,1024]{1,0:T(8,128)} reshape(f32[4,256,16,64]{3,2,1,0:T(8,128)} %copy.71) | data formatting | bytes 8388608 | tf_op jit(solution)/shard_map/reshape | solution.py:103
  248.3 18.6 %multiply_reduce_fusion = (f32[1024]{0:T(1024)S(1)}, f32[1024,1024]{1,0:T(8,128)}) fusion(bf16[4096,1024]{1,0:T(8,128)(2,1)} %param.16, bf16[1024,4096]{1,0:T(8,128)(2,1)} %all-gather.3.cloned.1.call-done, f32[4096]{0:T(1024)S(1)} %copy-done.4, f32[1024]{0:T(1024)S(1)} %add_rsqrt_fusion.1, f32[1024,1024]{1,0:T(8,128)} %reshape.81, ...), kind=kOutput, calls=%fused_computation.40 | convolution fusion | flops 8618245120 | bytes 29388800 | tf_op jit(solution)/shard_map/dot_general | solution.py:47
  266.9 11.8 %psum.7 = f32[1024]{0:T(1024)S(1)} all-reduce(f32[1024]{0:T(1024)S(1)} %get-tuple-element.55), channel_id=1, replica_groups=mesh['seq'=4,'chan'=8] {'chan'}, use_global_device_ids=true, to_apply=%region_5.6 | all-reduce | flops 1024 | bytes 8192 | tf_op jit(solution)/shard_map/psum | solution.py:105
  278.7 16.1 %fusion.30 = f32[1024,4096]{1,0:T(8,128)} fusion(bf16[1024,4096]{1,0:T(8,128)(2,1)} %param.25, f32[1024,1024]{1,0:T(8,128)} %get-tuple-element.56, f32[1024]{0:T(1024)S(1)} %copy-done.5, f32[1024]{0:T(1024)S(1)} %add_rsqrt_fusion), kind=kOutput, calls=%fused_computation.42 | convolution fusion | flops 8593080320 | bytes 29368320 | tf_op jit(solution)/shard_map/dot_general | solution.py:108
  294.8 116.4 %reduce-scatter.2.cloned.1.call-done = f32[1024,512]{1,0:T(8,128)} async-done(((f32[1024,4096]{1,0:T(8,128)}), f32[1024,512]{1,0:T(8,128)}) %reduce-scatter.2.cloned.1.call-update) | async-done | bytes 2097168 | tf_op jit(solution)/shard_map/reduce_scatter | solution.py:109
  411.2 2.9 add_convert_fusion
  (55 shorter events, 6.5 us)
Async XLA Ops:
  6.5 61.3 %all-gather.3.cloned.1.call-start = ((), (), s32[]{:S(2)}) async-start(), calls=%async_computation.1 | async-start | bytes 9437184 | tf_op jit(solution)/shard_map/all_gather | solution.py:43
  7.3 94.7 %all-gather.5.cloned.1.call-start = ((), (), s32[]{:S(2)}) async-start(), calls=%async_computation.2 | async-start | bytes 3538944 | tf_op jit(solution)/shard_map/all_gather | solution.py:53
  8.0 403.2 %reduce-scatter.2.cloned.1.call-start = ((), (), s32[]{:S(2)}) async-start(), calls=%async_computation.3 | async-start | bytes 18874368 | tf_op jit(solution)/shard_map/reduce_scatter | solution.py:109
  11.3 90.6 %copy-start.4 = (f32[4096]{0:T(1024)S(1)}, f32[4096]{0:T(1024)}, u32[]{:S(2)}) copy-start(f32[4096]{0:T(1024)} %param.15) | copy-start | bytes 49156
  72.9 37.6 %copy-start.3 = (f32[16]{0:T(128)S(1)}, f32[16]{0:T(128)}, u32[]{:S(2)}) copy-start(f32[16]{0:T(128)} %param.22) | copy-start | bytes 196
  126.6 9.8 %collective-permute-start.1 = (bf16[3,1024]{1,0:T(4,128)(2,1)S(1)}, bf16[3,1024]{1,0:T(4,128)(2,1)S(1)}, u32[]{:S(2)}, u32[]{:S(2)}) collective-permute-start(bf16[3,1024]{1,0:T(4,128)(2,1)S(1)} %slice.162), channel_id=1, source_target_pairs={{0,8},{8,16},{16,24},{1,9},{9,17},{17,25},{2,10},{10,18},{18,26},{... | collective-permute-start | bytes 18440 | tf_op jit(solution)/shard_map/ppermute | solution.py:17
  130.0 4.7 %collective-permute-start.2 = (f32[3,256]{1,0:T(4,128)S(1)}, f32[3,256]{1,0:T(4,128)S(1)}, u32[]{:S(2)}, u32[]{:S(2)}) collective-permute-start(f32[3,256]{1,0:T(4,128)S(1)} %slice.92), channel_id=1, source_target_pairs={{0,8},{8,16},{16,24},{1,9},{9,17},{17,25},{2,10},{10,18},{18,26},{... | collective-permute-start | bytes 9224 | tf_op jit(solution)/shard_map/ppermute | solution.py:17
  134.1 2.3 copy-start.1
  160.3 14.3 %collective-permute-start = (f32[16,128,64]{1,2,0:T(8,128)S(1)}, f32[16,128,64]{1,2,0:T(8,128)S(1)}, u32[]{:S(2)}, u32[]{:S(2)}) collective-permute-start(f32[16,128,64]{1,2,0:T(8,128)S(1)} %multiply_add_fusion.2), channel_id=1, source_target_pairs={{0,8},{8,16},{16,24},{1,9},{9,17},{17,25},{2,10},{10,18},{18,26},{... | collective-permute-start | bytes 1572872 | tf_op jit(solution)/shard_map/while/body/eval_jaxpr/ppermute | solution.py:17
  174.7 13.7 %collective-permute-start = (f32[16,128,64]{1,2,0:T(8,128)S(1)}, f32[16,128,64]{1,2,0:T(8,128)S(1)}, u32[]{:S(2)}, u32[]{:S(2)}) collective-permute-start(f32[16,128,64]{1,2,0:T(8,128)S(1)} %multiply_add_fusion.2), channel_id=1, source_target_pairs={{0,8},{8,16},{16,24},{1,9},{9,17},{17,25},{2,10},{10,18},{18,26},{... | collective-permute-start | bytes 1572872 | tf_op jit(solution)/shard_map/while/body/eval_jaxpr/ppermute | solution.py:17
  188.5 12.8 %collective-permute-start = (f32[16,128,64]{1,2,0:T(8,128)S(1)}, f32[16,128,64]{1,2,0:T(8,128)S(1)}, u32[]{:S(2)}, u32[]{:S(2)}) collective-permute-start(f32[16,128,64]{1,2,0:T(8,128)S(1)} %multiply_add_fusion.2), channel_id=1, source_target_pairs={{0,8},{8,16},{16,24},{1,9},{9,17},{17,25},{2,10},{10,18},{18,26},{... | collective-permute-start | bytes 1572872 | tf_op jit(solution)/shard_map/while/body/eval_jaxpr/ppermute | solution.py:17
  208.5 3.5 copy-start
  248.3 30.4 %copy-start.5 = (f32[1024]{0:T(1024)S(1)}, f32[1024]{0:T(1024)}, u32[]{:S(2)}) copy-start(f32[1024]{0:T(1024)} %param.24) | copy-start | bytes 12292
  294.8 116.4 %copy-start.2 = (bf16[1024,512]{1,0:T(8,128)(2,1)S(1)}, bf16[1024,512]{1,0:T(8,128)(2,1)}, u32[]{:S(2)}) copy-start(bf16[1024,512]{1,0:T(8,128)(2,1)} %param.14) | copy-start | bytes 3145732
Sparse Core Ops, SparseCore 0:
  9.2 58.5 all-gather.2
  69.7 32.1 all-gather.4
  294.9 116.1 reduce-scatter.1
where the time goes:
time: 428 us; the launch traced here: 421 us
  waiting for transfers between devices  232 us (54%)
  matrix products  95.4 us (22%)
  local copies, waits for them, and re-layouts  30.6 us (7%)
  starting transfers between devices  20.4 us (5%)
  other arithmetic  17.1 us (4%)
  between operations  13.6 us (3%)
  blocking collectives  11.8 us (3%)
    reduce_scatter x1, waiting for transfers between devices, local(): lax.psum_scatter(partial_out, 'chan', scatter_dimension=1, tiled=True)  116 us
    all_gather x1, waiting for transfers between devices, local(): gathered = lax.all_gather(tokens, 'chan', axis=1, tiled=True)  56.5 us
    all_gather x1, waiting for transfers between devices, local(): lax.all_gather(state_proj, 'chan', axis=0, tiled=True)  29 us
    ppermute x5, waiting for transfers between devices, from_behind(): lax.ppermute(value, axis, [(source, source + steps) for source in range(l...  28.3 us
    dot_general x1, matrix products, local(): local_out = jnp.einsum('chts,cshp->cthp', mixing, values, precision=precise)  20.5 us
    ppermute x5, starting transfers between devices, from_behind(): lax.ppermute(value, axis, [(source, source + steps) for source in range(l...  20.4 us
    dot_general x1, matrix products, local(): jnp.dot(normed, gate_proj, preferred_element_type=jnp.float32)  18.6 us
    dot_general x1, matrix products, local(): partial_out = jnp.dot(shaped, out_proj, preferred_element_type=jnp.float32)  16.1 us
  transfers between devices with their start and end apart: 8, of which 7 were waited for; matrix products, arithmetic and copies ran while one was open for 2% of the time, Pallas kernels for 0%

commit v1 on v0

--- a/solution.py
+++ b/solution.py
@@ -50,7 +50,9 @@
     start_head = lax.axis_index("chan") * heads
     projected = jnp.dot(
         normed,
-        lax.all_gather(state_proj, "chan", axis=0, tiled=True),
+        jnp.concatenate(
+            lax.all_to_all(jnp.stack([state_proj] * lax.axis_size("chan")), "chan", 0, 0), axis=0
+        ),
         preferred_element_type=jnp.float32,
     )
     state_raw = projected[:, : 2 * N]

time: 428 us -> 422 us (0.986)
  waiting for transfers between devices: 232 us -> 221 us
  starting transfers between devices: 20.4 us -> 25.6 us
    all_gather x1 -> x0, waiting for transfers between devices: 29 us -> none  [local(): lax.all_gather(state_proj, 'chan', axis=0, tiled=True)]
    all_gather x1, waiting for transfers between devices: 56.5 us -> 76.4 us  [local(): gathered = lax.all_gather(tokens, 'chan', axis=1, tiled=True)]
    all_to_all x0 -> x1, starting transfers between devices: none -> 5.2 us  [local(): lax.all_to_all(jnp.stack([state_proj] * lax.axis_size('chan')), 'chan', 0...]
  transfers between devices with their start and end apart: 8 -> 8, of which waited for: 7 -> 6; matrix products, arithmetic and copies ran while one was open for 2% -> 2% of each run, Pallas kernels for 0% -> 0%
where the time goes in v1:
time: 422 us; the launch traced here: 415 us
  waiting for transfers between devices  221 us (52%)
  matrix products  94.4 us (22%)
  local copies, waits for them, and re-layouts  31.3 us (7%)
  starting transfers between devices  25.6 us (6%)
  other arithmetic  16.5 us (4%)
  between operations  14 us (3%)
  blocking collectives  11.8 us (3%)
    reduce_scatter x1, waiting for transfers between devices, local(): lax.psum_scatter(partial_out, 'chan', scatter_dimension=1, tiled=True)  116 us
    all_gather x1, waiting for transfers between devices, local(): gathered = lax.all_gather(tokens, 'chan', axis=1, tiled=True)  76.4 us
    ppermute x5, waiting for transfers between devices, from_behind(): lax.ppermute(value, axis, [(source, source + steps) for source in range(l...  28.4 us
    dot_general x1, matrix products, local(): local_out = jnp.einsum('chts,cshp->cthp', mixing, values, precision=precise)  20.5 us
    ppermute x5, starting transfers between devices, from_behind(): lax.ppermute(value, axis, [(source, source + steps) for source in range(l...  20.4 us
    dot_general x1, matrix products, local(): jnp.dot(normed, gate_proj, preferred_element_type=jnp.float32)  18.6 us
    dot_general x1, matrix products, local(): partial_out = jnp.dot(shaped, out_proj, preferred_element_type=jnp.float32)  16.1 us
    reshape x2, local copies, waits for them, and re-layouts, local(): (local_out + carried_out).reshape(token_rows, heads * P_SIZE)  15.7 us
  transfers between devices with their start and end apart: 8, of which 6 were waited for; matrix products, arithmetic and copies ran while one was open for 2% of the time, Pallas kernels for 0%

profile of v1, /device:TPU:0, one launch (start us, length us, event | category | flops | bytes accessed | tf_op | source)
XLA Modules:
  0.0 414.9 jit_solution(12955484225790871171)
XLA Ops:
  6.5 0.7 all-gather.2.cloned.1.call-update
  7.3 3.0 stack.2
  10.3 5.2 %all-to-all-start = ((bf16[8,512,384]{2,1,0:T(8,128)(2,1)}), bf16[8,512,384]{2,1,0:T(8,128)(2,1)S(1)}, u32[]{:S(2)}, u32[]{:S(2)}) async-start(bf16[8,512,384]{2,1,0:T(8,128)(2,1)} %stack.2), calls=%async_computation | async-start | bytes 6291456 | tf_op jit(solution)/shard_map/all_to_all | solution.py:54
  15.9 76.4 %all-gather.2.cloned.1.call-done = bf16[1024,4096]{1,0:T(8,128)(2,1)} async-done(((bf16[1024,512]{1,0:T(8,128)(2,1)}), bf16[1024,4096]{1,0:T(8,128)(2,1)}) %all-gather.2.cloned.1.call-update) | async-done | bytes 8388624 | tf_op jit(solution)/shard_map/all_gather | solution.py:43
  92.2 5.1 %fusion = f32[1024]{0:T(1024)S(1)} fusion(bf16[1024,4096]{1,0:T(8,128)(2,1)} %all-gather.2.cloned.1.call-done), kind=kLoop, calls=%fused_computation.3 | loop fusion | flops 12581888 | bytes 8392704 | tf_op jit(solution)/shard_map/reduce_sum | solution.py:45
  97.4 7.1 %fusion.66 = f32[1024,384]{1,0:T(8,128)S(1)} fusion(bf16[4096,384]{1,0:T(8,128)(2,1)S(1)} %bitcast.80, bf16[1024,4096]{1,0:T(8,128)(2,1)} %all-gather.2.cloned.1.call-done, f32[4096]{0:T(1024)S(1)} %copy-done.7, f32[1024]{0:T(1024)S(1)} %add_rsqrt_fusion.1), kind=kOutput, calls=%fused_computation.96 | convolution fusion | flops 3238002688 | bytes 13127680 | tf_op jit(solution)/shard_map/dot_general | solution.py:51
  105.9 15.1 %fusion.73 = (f32[1024,1024]{1,0:T(8,128)}, bf16[1024,1024]{1,0:T(8,128)(2,1)S(1)}) fusion(bf16[4096,1024]{1,0:T(8,128)(2,1)} %param.17, bf16[1024,4096]{1,0:T(8,128)(2,1)} %all-gather.2.cloned.1.call-done, f32[4096]{0:T(1024)S(1)} %copy-done.7, f32[1024]{0:T(1024)S(1)} %add_rsqrt_fusion.1), kind=kOutput, calls=%fused_computation.101 | convolution fusion | flops 8608808960 | bytes 23089152 | tf_op jit(solution)/shard_map/dot_general | solution.py:48
  121.0 3.4 collective-permute-start.1
  124.4 3.9 collective-permute-start.2
  129.9 1.0 fusion.74
  130.9 3.9 divide_multiply_fusion
  134.8 5.3 %copy.47 = f32[1024,1024]{0,1:T(8,128)} copy(f32[1024,1024]{1,0:T(8,128)} %divide_multiply_fusion) | data formatting | bytes 8388608 | tf_op jit(solution)/shard_map/jit(silu)/mul | solution.py:26
  140.1 5.6 %reshape.73 = f32[4,256,16,64]{1,0,3,2:T(4,128)} reshape(f32[1024,1024]{0,1:T(8,128)} %copy.47) | data formatting | bytes 8388608 | tf_op jit(solution)/shard_map/reshape | solution.py:69
  145.8 3.3 broadcast_multiply_fusion
  149.1 5.4 %fusion.31 = (f32[16,128,64]{1,2,0:T(8,128)S(1)}, f32[4,16,64,128]{3,2,1,0:T(8,128)}) fusion(f32[16,4]{0,1:T(4,128)S(1)} %get-tuple-element.50, f32[4,256,128,1]{2,1,3,0:T(8,128)S(1)} %bitcast.78, f32[4,256,16,64]{1,0,3,2:T(4,128)S(1)} %broadcast_multiply_fusion), kind=kOutput, calls=%fused_computation.44 | convolution fusion | flops 1611530240 | bytes 7340288 | tf_op jit(solution)/shard_map/csn,cshp->chnp/dot_general | solution.py:83
  154.6 41.4 %while.10 = (s32[]{:T(128)}, f32[16,128,64]{1,2,0:T(8,128)S(1)}, f32[16]{0:T(128)S(1)}, f32[16,128,64]{1,2,0:T(8,128)S(1)}, s32[]{:T(128)}) while((s32[]{:T(128)}, f32[16,128,64]{1,2,0:T(8,128)S(1)}, f32[16]{0:T(128)S(1)}, f32[16,128,64]{1,2,0:T(8,128)S(1)}, s32[]{:T(128)}) %tuple.31), condition=%wide.region_3.4_spmd, body=%wide.region_2.3_spmd.sunk | while | flops 262146 | bytes 3670181 | solution.py:100
  154.7 4.2 %collective-permute-start = (f32[16,128,64]{1,2,0:T(8,128)S(1)}, f32[16,128,64]{1,2,0:T(8,128)S(1)}, u32[]{:S(2)}, u32[]{:S(2)}) collective-permute-start(f32[16,128,64]{1,2,0:T(8,128)S(1)} %multiply_add_fusion.2), channel_id=1, source_target_pairs={{0,8},{8,16},{16,24},{1,9},{9,17},{17,25},{2,10},{10,18},{18,26},{... | collective-permute-start | bytes 1572872 | tf_op jit(solution)/shard_map/while/body/eval_jaxpr/ppermute | solution.py:17
  158.9 10.1 %collective-permute-done = f32[16,128,64]{1,2,0:T(8,128)S(1)} collective-permute-done((f32[16,128,64]{1,2,0:T(8,128)S(1)}, f32[16,128,64]{1,2,0:T(8,128)S(1)}, u32[]{:S(2)}, u32[]{:S(2)}) %collective-permute-start) | collective-permute-done | bytes 524320 | tf_op jit(solution)/shard_map/while/body/eval_jaxpr/ppermute | solution.py:17
  169.2 4.4 %collective-permute-start = (f32[16,128,64]{1,2,0:T(8,128)S(1)}, f32[16,128,64]{1,2,0:T(8,128)S(1)}, u32[]{:S(2)}, u32[]{:S(2)}) collective-permute-start(f32[16,128,64]{1,2,0:T(8,128)S(1)} %multiply_add_fusion.2), channel_id=1, source_target_pairs={{0,8},{8,16},{16,24},{1,9},{9,17},{17,25},{2,10},{10,18},{18,26},{... | collective-permute-start | bytes 1572872 | tf_op jit(solution)/shard_map/while/body/eval_jaxpr/ppermute | solution.py:17
  173.6 9.3 %collective-permute-done = f32[16,128,64]{1,2,0:T(8,128)S(1)} collective-permute-done((f32[16,128,64]{1,2,0:T(8,128)S(1)}, f32[16,128,64]{1,2,0:T(8,128)S(1)}, u32[]{:S(2)}, u32[]{:S(2)}) %collective-permute-start) | collective-permute-done | bytes 524320 | tf_op jit(solution)/shard_map/while/body/eval_jaxpr/ppermute | solution.py:17
  183.0 4.4 %collective-permute-start = (f32[16,128,64]{1,2,0:T(8,128)S(1)}, f32[16,128,64]{1,2,0:T(8,128)S(1)}, u32[]{:S(2)}, u32[]{:S(2)}) collective-permute-start(f32[16,128,64]{1,2,0:T(8,128)S(1)} %multiply_add_fusion.2), channel_id=1, source_target_pairs={{0,8},{8,16},{16,24},{1,9},{9,17},{17,25},{2,10},{10,18},{18,26},{... | collective-permute-start | bytes 1572872 | tf_op jit(solution)/shard_map/while/body/eval_jaxpr/ppermute | solution.py:17
  187.4 8.4 %collective-permute-done = f32[16,128,64]{1,2,0:T(8,128)S(1)} collective-permute-done((f32[16,128,64]{1,2,0:T(8,128)S(1)}, f32[16,128,64]{1,2,0:T(8,128)S(1)}, u32[]{:S(2)}, u32[]{:S(2)}) %collective-permute-start) | collective-permute-done | bytes 524320 | tf_op jit(solution)/shard_map/while/body/eval_jaxpr/ppermute | solution.py:17
  196.0 6.7 %bitcast_add_fusion.1 = f32[4,16,128,64]{2,0,3,1:T(4,128)S(1)} fusion(f32[4,16,128,64]{2,3,1,0:T(8,128)} %bitcast.73, f32[16,128,64]{1,2,0:T(8,128)S(1)} %get-tuple-element.27, f32[4,16]{0,1:T(8,128)S(1)} %copy.58, f32[4,16]{0,1:T(8,128)S(1)} %copy.56, f32[4,16]{0,1:T(8,128)S(1)} %copy.55, pred[4,4]{1,0:T(4,128)(4,1)S(1)} %iota_compare_fusion.1), kind=kOutput, calls=%fused_computation.45 | convolution fusion | flops 26214912 | bytes 4719376 | tf_op jit(solution)/shard_map/cdh,dhnp->chnp/dot_general | solution.py:91
  203.0 3.5 fusion.75
  206.5 20.5 %bitcast_add_fusion = f32[4,256,16,64]{1,3,2,0:T(8,128)} fusion(f32[4,256,16,64]{1,3,2,0:T(8,128)S(1)} %bitcast.79, f32[4,256,16]{1,2,0:T(8,128)S(1)} %exponential_bitcast_fusion, f32[4,16,256]{2,1,0:T(8,128)S(1)} %copy.50, f32[4,16,256]{2,1,0:T(8,128)S(1)} %fusion.51, f32[4,256,256]{2,1,0:T(8,128)S(1)} %fusion.74, ...), kind=kOutput, calls=%fused_computation.35 | convolution fusion | flops 3240099840 | bytes 13893632 | tf_op jit(solution)/shard_map/chts,cshp->cthp/dot_general | solution.py:80
  227.1 8.0 %copy.71 = f32[4,256,16,64]{3,2,1,0:T(8,128)} copy(f32[4,256,16,64]{1,3,2,0:T(8,128)} %bitcast_add_fusion) | data formatting | bytes 8388608 | tf_op jit(solution)/shard_map/reshape | solution.py:105
  235.1 7.7 %reshape.87 = f32[1024,1024]{1,0:T(8,128)} reshape(f32[4,256,16,64]{3,2,1,0:T(8,128)} %copy.71) | data formatting | bytes 8388608 | tf_op jit(solution)/shard_map/reshape | solution.py:105
  242.8 18.6 %multiply_reduce_fusion = (f32[1024]{0:T(1024)S(1)}, f32[1024,1024]{1,0:T(8,128)}) fusion(bf16[4096,1024]{1,0:T(8,128)(2,1)} %param.16, bf16[1024,4096]{1,0:T(8,128)(2,1)} %all-gather.2.cloned.1.call-done, f32[4096]{0:T(1024)S(1)} %copy-done.7, f32[1024]{0:T(1024)S(1)} %add_rsqrt_fusion.1, f32[1024,1024]{1,0:T(8,128)} %reshape.87, ...), kind=kOutput, calls=%fused_computation.40 | convolution fusion | flops 8618245120 | bytes 29388800 | tf_op jit(solution)/shard_map/dot_general | solution.py:47
  261.3 11.8 %psum.7 = f32[1024]{0:T(1024)S(1)} all-reduce(f32[1024]{0:T(1024)S(1)} %get-tuple-element.55), channel_id=1, replica_groups=mesh['seq'=4,'chan'=8] {'chan'}, use_global_device_ids=true, to_apply=%region_5.6 | all-reduce | flops 1024 | bytes 8192 | tf_op jit(solution)/shard_map/psum | solution.py:107
  273.2 16.1 %fusion.30 = f32[1024,4096]{1,0:T(8,128)} fusion(bf16[1024,4096]{1,0:T(8,128)(2,1)} %param.25, f32[1024,1024]{1,0:T(8,128)} %get-tuple-element.56, f32[1024]{0:T(1024)S(1)} %copy-done.8, f32[1024]{0:T(1024)S(1)} %add_rsqrt_fusion), kind=kOutput, calls=%fused_computation.42 | convolution fusion | flops 8593080320 | bytes 29368320 | tf_op jit(solution)/shard_map/dot_general | solution.py:110
  289.3 115.6 %reduce-scatter.2.cloned.1.call-done = f32[1024,512]{1,0:T(8,128)} async-done(((f32[1024,4096]{1,0:T(8,128)}), f32[1024,512]{1,0:T(8,128)}) %reduce-scatter.2.cloned.1.call-update) | async-done | bytes 2097168 | tf_op jit(solution)/shard_map/reduce_scatter | solution.py:111
  404.9 2.9 add_convert_fusion
  (63 shorter events, 3.8 us)
Async XLA Ops:
  6.5 85.7 %all-gather.2.cloned.1.call-start = ((), (), s32[]{:S(2)}) async-start(), calls=%async_computation.2 | async-start | bytes 9437184 | tf_op jit(solution)/shard_map/all_gather | solution.py:43
  7.3 8.3 %copy-start.6 = (f32[16]{0:T(128)S(1)}, f32[16]{0:T(128)}, u32[]{:S(2)}) copy-start(f32[16]{0:T(128)} %param.23) | copy-start | bytes 196
  7.3 8.5 %copy-start.9 = (f32[16]{0:T(128)S(1)}, f32[16]{0:T(128)}, u32[]{:S(2)}) copy-start(f32[16]{0:T(128)} %param.21) | copy-start | bytes 196
  7.3 8.5 %copy-start.4 = (f32[4,256]{1,0:T(4,128)S(1)}, f32[4,256]{1,0:T(4,128)}, u32[]{:S(2)}) copy-start(f32[4,256]{1,0:T(4,128)} %param.20) | copy-start | bytes 12292
  7.3 8.5 %copy-start.3 = (f32[4,1024]{1,0:T(4,128)S(1)}, f32[4,1024]{1,0:T(4,128)}, u32[]{:S(2)}) copy-start(f32[4,1024]{1,0:T(4,128)} %param.19) | copy-start | bytes 49156
  10.3 87.0 %all-to-all-start = ((bf16[8,512,384]{2,1,0:T(8,128)(2,1)}), bf16[8,512,384]{2,1,0:T(8,128)(2,1)S(1)}, u32[]{:S(2)}, u32[]{:S(2)}) async-start(bf16[8,512,384]{2,1,0:T(8,128)(2,1)} %stack.2), calls=%async_computation | async-start | bytes 6291456 | tf_op jit(solution)/shard_map/all_to_all | solution.py:54
  15.5 389.4 %reduce-scatter.2.cloned.1.call-start = ((), (), s32[]{:S(2)}) async-start(), calls=%async_computation.3 | async-start | bytes 18874368 | tf_op jit(solution)/shard_map/reduce_scatter | solution.py:111
  15.8 81.5 %copy-start.7 = (f32[4096]{0:T(1024)S(1)}, f32[4096]{0:T(1024)}, u32[]{:S(2)}) copy-start(f32[4096]{0:T(1024)} %param.15) | copy-start | bytes 49156
  97.3 7.6 %copy-start.5 = (f32[16]{0:T(128)S(1)}, f32[16]{0:T(128)}, u32[]{:S(2)}) copy-start(f32[16]{0:T(128)} %param.22) | copy-start | bytes 196
  121.0 9.8 %collective-permute-start.1 = (bf16[3,1024]{1,0:T(4,128)(2,1)S(1)}, bf16[3,1024]{1,0:T(4,128)(2,1)S(1)}, u32[]{:S(2)}, u32[]{:S(2)}) collective-permute-start(bf16[3,1024]{1,0:T(4,128)(2,1)S(1)} %slice.162), channel_id=1, source_target_pairs={{0,8},{8,16},{16,24},{1,9},{9,17},{17,25},{2,10},{10,18},{18,26},{... | collective-permute-start | bytes 18440 | tf_op jit(solution)/shard_map/ppermute | solution.py:17
  124.4 4.7 %collective-permute-start.2 = (f32[3,256]{1,0:T(4,128)S(1)}, f32[3,256]{1,0:T(4,128)S(1)}, u32[]{:S(2)}, u32[]{:S(2)}) collective-permute-start(f32[3,256]{1,0:T(4,128)S(1)} %slice.92), channel_id=1, source_target_pairs={{0,8},{8,16},{16,24},{1,9},{9,17},{17,25},{2,10},{10,18},{18,26},{... | collective-permute-start | bytes 9224 | tf_op jit(solution)/shard_map/ppermute | solution.py:17
  128.6 2.3 copy-start.1
  154.7 14.4 %collective-permute-start = (f32[16,128,64]{1,2,0:T(8,128)S(1)}, f32[16,128,64]{1,2,0:T(8,128)S(1)}, u32[]{:S(2)}, u32[]{:S(2)}) collective-permute-start(f32[16,128,64]{1,2,0:T(8,128)S(1)} %multiply_add_fusion.2), channel_id=1, source_target_pairs={{0,8},{8,16},{16,24},{1,9},{9,17},{17,25},{2,10},{10,18},{18,26},{... | collective-permute-start | bytes 1572872 | tf_op jit(solution)/shard_map/while/body/eval_jaxpr/ppermute | solution.py:17
  169.2 13.7 %collective-permute-start = (f32[16,128,64]{1,2,0:T(8,128)S(1)}, f32[16,128,64]{1,2,0:T(8,128)S(1)}, u32[]{:S(2)}, u32[]{:S(2)}) collective-permute-start(f32[16,128,64]{1,2,0:T(8,128)S(1)} %multiply_add_fusion.2), channel_id=1, source_target_pairs={{0,8},{8,16},{16,24},{1,9},{9,17},{17,25},{2,10},{10,18},{18,26},{... | collective-permute-start | bytes 1572872 | tf_op jit(solution)/shard_map/while/body/eval_jaxpr/ppermute | solution.py:17
  183.0 12.8 %collective-permute-start = (f32[16,128,64]{1,2,0:T(8,128)S(1)}, f32[16,128,64]{1,2,0:T(8,128)S(1)}, u32[]{:S(2)}, u32[]{:S(2)}) collective-permute-start(f32[16,128,64]{1,2,0:T(8,128)S(1)} %multiply_add_fusion.2), channel_id=1, source_target_pairs={{0,8},{8,16},{16,24},{1,9},{9,17},{17,25},{2,10},{10,18},{18,26},{... | collective-permute-start | bytes 1572872 | tf_op jit(solution)/shard_map/while/body/eval_jaxpr/ppermute | solution.py:17
  203.0 3.5 copy-start
  242.8 30.4 %copy-start.8 = (f32[1024]{0:T(1024)S(1)}, f32[1024]{0:T(1024)}, u32[]{:S(2)}) copy-start(f32[1024]{0:T(1024)} %param.24) | copy-start | bytes 12292
  289.2 115.6 %copy-start.2 = (bf16[1024,512]{1,0:T(8,128)(2,1)S(1)}, bf16[1024,512]{1,0:T(8,128)(2,1)}, u32[]{:S(2)}) copy-start(bf16[1024,512]{1,0:T(8,128)(2,1)} %param.14) | copy-start | bytes 3145732
Sparse Core Ops, SparseCore 0:
  9.2 82.9 all-gather.1
  289.4 115.4 reduce-scatter.1
